TPU v7x, 32 devices: a whole 2x2x4 slice. The times are simulated.
32 devices in a mesh: tm: 8 (over z, y), col: 4 (over x, core).
Axes of the slice: x: 2, y: 2, z: 4, core: 2. Of those that a mesh axis runs over, the one named last changes fastest.
Arguments:
- block_values: bfloat16 [4, 16384, 128], P('col', 'tm'), may hold values from -6 to 6
- block_shifts: bfloat16 [4, 16384, 128], P('col', 'tm'), may hold values from -1 to 1
- block_sensor: int32 [4, 16384], P('col', 'tm'), may hold values from 0 to 4095
- block_window: int32 [4, 16384], P('col', 'tm'), may hold values from 0 to 3
- block_owner: int32 [4, 16384, 1], P('col', 'tm'), may hold values from 0 to 7; in each aligned block of 2048 rows (0 to 2047, 2048 to 4095, ..., all dimensions but the last counted through in order) at most 384 rows name the same one
- block_counts: int32 [4, 8], P('col', 'tm'), may hold values from 1536 to 2048
- calibration: bfloat16 [16384, 4096], P('tm', 'col'), may hold values from -0.046875 to 0.046875
Outputs:
- calibrated: bfloat16 [4096, 4096], P('tm', 'col')
Inputs may be any that keep to these rules, and one draw needn't show every extreme that they name: `block_owner`: among the 2048 block slots of one device, at most 384 name the same owner, a bound that some block reaches. The live blocks of device (tm t, col c) are its first block_counts[c, t] slots.
All inputs are finite; a program needn't handle non-finite values.
Results may differ from a plain program's by a relative error of at most 0.015.
Values may be sent and summed in bfloat16 or wider, within the bound.
A program may use at most 128 MiB of HBM per device.

v0:
```python
import jax
import jax.numpy as jnp
from jax import lax
from jax.sharding import PartitionSpec as P

SENSORS = 16384
ROWS_DEV = 512


def spread_samples(values, shifts):
    samples = values.astype(jnp.float32)
    offsets = shifts.astype(jnp.float32)
    result = jnp.zeros(samples.shape, jnp.float32)
    lead = [(0, 0)] * (samples.ndim - 1)
    for displace in (-1, 0, 1):
        weight = jnp.maximum(0.0, 1.0 - jnp.abs(offsets - displace)).astype(jnp.bfloat16)
        weight = lax.optimization_barrier(weight).astype(jnp.float32)
        product = weight * samples
        if displace == 1:
            result = result + jnp.pad(product[..., :-1], lead + [(1, 0)])
        elif displace == -1:
            result = jnp.pad(product[..., 1:], lead + [(0, 1)])
        else:
            result = result + product
    return result


def spread_slots(moved_slots):
    return spread_samples(moved_slots[:, :, 0], moved_slots[:, :, 1])


def per_device(
    block_values, block_shifts, block_sensor, block_window, block_owner, block_counts, calibration
):
    values = block_values[0]
    shifts = block_shifts[0]
    blocks = values.shape[0]
    length = values.shape[1]
    owners = lax.axis_size("tm")
    group_size = SENSORS // lax.axis_size("col")
    windows = ROWS_DEV // length
    capacity = blocks * 3 // (2 * owners)
    slot_total = owners * capacity
    block_index = lax.iota(jnp.int32, blocks)
    is_live = block_index < block_counts[0, 0]
    values = jnp.where(is_live[:, None], values, jnp.zeros_like(values))
    owner_ids = block_owner[0, :, 0]
    owner_onehot = (owner_ids[:, None] == lax.iota(jnp.int32, owners)[None, :]).astype(jnp.bfloat16)
    lower_mask = (block_index[:, None] > block_index[None, :]).astype(jnp.bfloat16)
    earlier = jnp.dot(lower_mask, owner_onehot, preferred_element_type=jnp.float32)
    slot_rank = jnp.sum(earlier * owner_onehot.astype(jnp.float32), axis=1).astype(jnp.int32)
    slot_index = owner_ids * capacity + slot_rank
    slot_match = slot_index[None, :] == lax.iota(jnp.int32, slot_total)[:, None]
    source = jnp.max(jnp.where(slot_match, block_index[None, :], -1), axis=1)
    filled = source >= 0
    source_row = jnp.maximum(source, 0)
    row_keys = block_window[0] * group_size + block_sensor[0]
    payload = jnp.stack((values, shifts), axis=1)
    outgoing = jnp.where(
        filled[:, None, None], jnp.take(payload, source_row, axis=0), jnp.zeros((), jnp.bfloat16)
    )
    outgoing = outgoing.reshape(owners, capacity, 2, length)
    outgoing_keys = jnp.where(filled, jnp.take(row_keys, source_row, axis=0), 0).reshape(
        owners, capacity
    )
    contribution = spread_slots(
        lax.all_to_all(outgoing, "tm", split_axis=0, concat_axis=0, tiled=True)
    )
    incoming_keys = lax.all_to_all(outgoing_keys, "tm", split_axis=0, concat_axis=0, tiled=True)
    flat_keys = incoming_keys.reshape(-1)
    flat_contrib = contribution.reshape(-1, length)
    upper_part = flat_contrib.astype(jnp.bfloat16)
    lower_part = (flat_contrib - upper_part.astype(jnp.float32)).astype(jnp.bfloat16)
    sensor_iota = lax.iota(jnp.int32, group_size)
    window_rows = []
    for window in range(windows):
        target = flat_keys - window * group_size
        place_onehot = (target[:, None] == sensor_iota[None, :]).astype(jnp.bfloat16)
        dims = (((0,), (0,)), ((), ()))
        window_sum = lax.dot_general(
            upper_part, place_onehot, dims, preferred_element_type=jnp.float32
        )
        window_sum = window_sum + lax.dot_general(
            lower_part, place_onehot, dims, preferred_element_type=jnp.float32
        )
        window_rows.append(window_sum)
    aligned = jnp.concatenate(window_rows, axis=0).astype(jnp.bfloat16)
    gathered = lax.all_gather(aligned, "col", axis=1, tiled=True)
    regrouped = lax.all_to_all(gathered, "tm", split_axis=1, concat_axis=0, tiled=True)
    return lax.psum_scatter(
        jnp.dot(regrouped, calibration, preferred_element_type=jnp.float32).astype(jnp.bfloat16),
        "tm",
        scatter_dimension=0,
        tiled=True,
    )


def solution(mesh):
    placed = (
        P("col", "tm", None),
        P("col", "tm", None),
        P("col", "tm"),
        P("col", "tm"),
        P("col", "tm", None),
        P("col", "tm"),
        P("tm", "col"),
    )
    return jax.shard_map(
        per_device, mesh=mesh, in_specs=placed, out_specs=P("tm", "col"), check_vma=False
    )
```

profile of v0, /device:TPU:0, one launch (start us, length us, event | category | flops | bytes accessed | tf_op | source)
XLA Modules:
  0.0 889.2 jit_solution(16694593911328433421)
XLA Ops:
  6.5 2.2 fusion.38
  8.8 0.0 copy-done.4
  8.8 3.4 select_reduce_fusion
  12.2 0.0 copy-done.5
  12.2 0.0 copy-done.6
  12.3 0.0 copy-start.2
  12.3 0.0 copy-start.3
  12.3 17.4 %gather_fusion.1 = s32[3072]{0:T(1024)S(1)} fusion(s32[2048]{0:T(1024)S(1)} %bitcast.39, s32[3072]{0:T(1024)S(1)} %maximum_clamp_fusion), kind=kCustom, calls=%fused_computation.1 | custom fusion | bytes 36864 | tf_op jit(solution)/shard_map/jit(_take)/gather | solution.py:63
  29.7 0.6 select_select_fusion
  30.3 7.5 all-to-all-start.1
  38.6 0.0 copy-done.2
  38.6 8.1 copy.15
  46.7 0.0 copy-done.3
  46.7 15.2 %broadcast_select_fusion.2 = bf16[2048,1,128]{2,1,0:T(2,128)(2,1)S(1)} fusion(pred[2048]{0:T(1024)(128)(4,1)S(1)} %iota_compare_fusion.37, bf16[2048,1,128]{2,0,1:T(8,128)(2,1)S(1)} %bitcast.47), kind=kLoop, calls=%fused_computation.43 | loop fusion | flops 262144 | bytes 1050624 | tf_op jit(solution)/shard_map/jit(_where)/select_n | solution.py:46
  61.9 2.4 pad_maximum_fusion.1
  64.4 10.4 %gather_fusion = bf16[3072,2,128]{2,1,0:T(2,128)(2,1)S(1)} fusion(bf16[2048,2,128]{2,1,0:T(2,128)(2,1)S(1)} %pad_maximum_fusion.1, s32[3072]{0:T(1024)S(1)} %maximum_clamp_fusion), kind=kCustom, calls=%fused_computation | custom fusion | bytes 3158016 | tf_op jit(solution)/shard_map/jit(_take)/gather | solution.py:60
  74.8 9.5 %broadcast_select_fusion.1 = bf16[8,384,2,128]{3,2,1,0:T(2,128)(2,1)} fusion(pred[8,384]{1,0:T(8,128)(4,1)S(1)} %ge.33, bf16[8,384,2,128]{3,2,1,0:T(2,128)(2,1)S(1)} %bitcast.45, pred[8,384]{1,0:T(8,128)(4,1)S(1)} %le.30), kind=kLoop, calls=%fused_computation.38 | loop fusion | flops 1572864 | bytes 3151872 | tf_op jit(solution)/shard_map/jit(_where)/select_n | solution.py:59
  84.2 0.0 all-to-all-done.1
  84.2 6.0 all-to-all-start
  90.2 0.0 all-gather.2.cloned.1.call-start
  90.3 36.4 %all-to-all-done = bf16[8,384,2,128]{3,2,1,0:T(2,128)(2,1)S(1)} async-done(((bf16[8,384,2,128]{3,2,1,0:T(2,128)(2,1)}), bf16[8,384,2,128]{3,2,1,0:T(2,128)(2,1)S(1)}, u32[]{:S(2)}, u32[]{:S(2)}) %all-to-all-start) | async-done | bytes 1572896 | tf_op jit(solution)/shard_map/all_to_all | solution.py:67
  126.7 2.6 fusion.44
  129.3 0.8 fusion.41
  130.1 0.7 slice_multiply_fusion.1
  130.9 0.6 pad_add_fusion
  131.4 0.2 fusion.37
  131.7 0.0 copy-start.1
  131.7 0.0 copy-start
  131.7 11.8 %fusion.6 = f32[128,4096]{1,0:T(8,128)} fusion(bf16[3072,128]{1,0:T(8,128)(2,1)S(1)} %get-tuple-element.8, s32[3072]{0:T(1024)S(1)} %bitcast.49), kind=kOutput, calls=%fused_computation.12 | convolution fusion | flops 3233808384 | bytes 2895872 | tf_op jit(solution)/shard_map/dot_general | solution.py:83
  143.5 11.9 %fusion = f32[128,4096]{1,0:T(8,128)} fusion(bf16[3072,128]{1,0:T(8,128)(2,1)S(1)} %get-tuple-element.8, s32[3072]{0:T(1024)S(1)} %get-tuple-element.18), kind=kOutput, calls=%fused_computation.3 | convolution fusion | flops 3233808384 | bytes 2895872 | tf_op jit(solution)/shard_map/dot_general | solution.py:83
  155.4 0.0 copy-done.1
  155.4 12.0 %fusion.2 = f32[128,4096]{1,0:T(8,128)} fusion(bf16[3072,128]{1,0:T(8,128)(2,1)S(1)} %get-tuple-element.8, s32[3072]{0:T(1024)S(1)} %get-tuple-element.19), kind=kOutput, calls=%fused_computation.6 | convolution fusion | flops 3233808384 | bytes 2895872 | tf_op jit(solution)/shard_map/dot_general | solution.py:83
  167.4 12.5 %fusion.21 = bf16[128,4096]{1,0:T(8,128)(2,1)S(1)} fusion(f32[128,4096]{1,0:T(8,128)} %fusion, bf16[3072,128]{1,0:T(8,128)(2,1)S(1)} %get-tuple-element.9, s32[3072]{0:T(1024)S(1)} %get-tuple-element.18), kind=kOutput, calls=%fused_computation.32 | convolution fusion | flops 3234856960 | bytes 3944448 | tf_op jit(solution)/shard_map/dot_general | solution.py:80
  180.0 0.0 copy-done
  180.0 12.3 %fusion.22 = bf16[128,4096]{1,0:T(8,128)(2,1)S(1)} fusion(f32[128,4096]{1,0:T(8,128)} %fusion.2, bf16[3072,128]{1,0:T(8,128)(2,1)S(1)} %get-tuple-element.9, s32[3072]{0:T(1024)S(1)} %get-tuple-element.19), kind=kOutput, calls=%fused_computation.33 | convolution fusion | flops 3234856960 | bytes 3944448 | tf_op jit(solution)/shard_map/dot_general | solution.py:80
  192.3 12.9 %fusion.4 = f32[128,4096]{1,0:T(8,128)} fusion(bf16[3072,128]{1,0:T(8,128)(2,1)} %copy-done.1, s32[3072]{0:T(1024)S(1)} %get-tuple-element.17), kind=kOutput, calls=%fused_computation.9 | convolution fusion | flops 3233808384 | bytes 2895872 | tf_op jit(solution)/shard_map/dot_general | solution.py:83
  205.2 12.6 %fusion.23 = bf16[128,4096]{1,0:T(8,128)(2,1)S(1)} fusion(f32[128,4096]{1,0:T(8,128)} %fusion.4, bf16[3072,128]{1,0:T(8,128)(2,1)} %copy-done, s32[3072]{0:T(1024)S(1)} %get-tuple-element.17), kind=kOutput, calls=%fused_computation.34 | convolution fusion | flops 3234856960 | bytes 3944448 | tf_op jit(solution)/shard_map/dot_general | solution.py:80
  217.8 13.6 %fusion.24 = bf16[128,4096]{1,0:T(8,128)(2,1)} fusion(f32[128,4096]{1,0:T(8,128)} %fusion.6, bf16[3072,128]{1,0:T(8,128)(2,1)} %copy-done, s32[3072]{0:T(1024)S(1)} %bitcast.50), kind=kOutput, calls=%fused_computation.35 | convolution fusion | flops 3234856960 | bytes 3944448 | tf_op jit(solution)/shard_map/dot_general | solution.py:80
  231.4 3.2 pad_maximum_fusion
  234.5 0.0 all-gather.2.cloned.1.call-update
  234.6 0.0 reduce-scatter.2.cloned.1.call-start
  234.6 105.0 %all-gather.2.cloned.1.call-done = bf16[512,16384]{1,0:T(8,128)(2,1)} async-done(((bf16[512,4096]{1,0:T(8,128)(2,1)}), bf16[512,16384]{1,0:T(8,128)(2,1)}) %all-gather.2.cloned.1.call-update) | async-done | bytes 16777232 | tf_op jit(solution)/shard_map/all_gather | solution.py:88
  339.7 8.0 copy.25
  347.7 0.0 copy-start.7
  347.7 368.8 %all_to_all.30 = bf16[512,8,2048]{2,0,1:T(8,128)(2,1)S(1)} all-to-all(bf16[512,8,2048]{2,0,1:T(8,128)(2,1)S(1)} %bitcast.40), channel_id=1, replica_groups=mesh['tm'=8,'col'=4] {'tm'}, dimensions={1} | all-to-all | bytes 33554432 | tf_op jit(solution)/shard_map/all_to_all | solution.py:89
  716.5 19.3 %convolution_convert_fusion = bf16[4096,1024]{1,0:T(8,128)(2,1)} fusion(bf16[4096,2048]{1,0:T(8,128)(2,1)S(1)} %bitcast.44, bf16[2048,1024]{1,0:T(8,128)(2,1)S(1)} %copy-done.7), kind=kOutput, calls=%fused_computation.27 | convolution fusion | flops 17184063488 | bytes 29360128 | tf_op jit(solution)/shard_map/dot_general | solution.py:91
  735.8 0.0 reduce-scatter.2.cloned.1.call-update
  735.8 146.2 %reduce-scatter.2.cloned.1.call-done = bf16[512,1024]{1,0:T(8,128)(2,1)} async-done(((bf16[4096,1024]{1,0:T(8,128)(2,1)}), bf16[512,1024]{1,0:T(8,128)(2,1)}) %reduce-scatter.2.cloned.1.call-update) | async-done | bytes 1048592 | tf_op jit(solution)/shard_map/reduce_scatter | solution.py:90
  (11 shorter events, 0.1 us)
Async XLA Ops:
  6.5 2.2 copy-start.4
  6.5 5.7 copy-start.5
  6.5 5.7 copy-start.6
  12.3 26.3 %copy-start.2 = (bf16[1,2048,128]{2,1,0:T(8,128)(2,1)S(1)}, bf16[1,2048,128]{2,1,0:T(8,128)(2,1)}, u32[]{:S(2)}) copy-start(bf16[1,2048,128]{2,1,0:T(8,128)(2,1)} %param.8) | copy-start | bytes 1572868
  12.3 34.5 %copy-start.3 = (bf16[1,2048,128]{2,1,0:T(8,128)(2,1)S(1)}, bf16[1,2048,128]{2,1,0:T(8,128)(2,1)}, u32[]{:S(2)}) copy-start(bf16[1,2048,128]{2,1,0:T(8,128)(2,1)} %param.7) | copy-start | bytes 1572868
  30.3 53.9 %all-to-all-start.1 = ((s32[8,1,384]{2,1,0:T(1,128)}), s32[8,1,384]{2,1,0:T(1,128)S(1)}, u32[]{:S(2)}, u32[]{:S(2)}) async-start(s32[8,1,384]{2,1,0:T(1,128)} %bitcast.11), calls=%async_computation.1 | async-start | bytes 24576 | tf_op jit(solution)/shard_map/all_to_all | solution.py:69
  84.2 42.5 %all-to-all-start = ((bf16[8,384,2,128]{3,2,1,0:T(2,128)(2,1)}), bf16[8,384,2,128]{3,2,1,0:T(2,128)(2,1)S(1)}, u32[]{:S(2)}, u32[]{:S(2)}) async-start(bf16[8,384,2,128]{3,2,1,0:T(2,128)(2,1)} %broadcast_select_fusion.1), calls=%async_computation | async-start | bytes 3145728 | tf_op jit(solution)/shard_map/all_to_all | solution.py:67
  90.2 249.4 %all-gather.2.cloned.1.call-start = ((), (), s32[]{:S(2)}) async-start(), calls=%async_computation.4 | async-start | bytes 20971520 | tf_op jit(solution)/shard_map/all_gather | solution.py:88
  131.7 23.8 %copy-start.1 = (bf16[3072,128]{1,0:T(8,128)(2,1)}, bf16[3072,128]{1,0:T(8,128)(2,1)S(1)}, u32[]{:S(2)}) copy-start(bf16[3072,128]{1,0:T(8,128)(2,1)S(1)} %get-tuple-element.8) | copy-start | bytes 2359300
  131.7 48.3 %copy-start = (bf16[3072,128]{1,0:T(8,128)(2,1)}, bf16[3072,128]{1,0:T(8,128)(2,1)S(1)}, u32[]{:S(2)}) copy-start(bf16[3072,128]{1,0:T(8,128)(2,1)S(1)} %get-tuple-element.9) | copy-start | bytes 2359300
  234.6 647.4 %reduce-scatter.2.cloned.1.call-start = ((), (), s32[]{:S(2)}) async-start(), calls=%async_computation.5 | async-start | bytes 9437184 | tf_op jit(solution)/shard_map/reduce_scatter | solution.py:90
  347.7 368.8 %copy-start.7 = (bf16[2048,1024]{1,0:T(8,128)(2,1)S(1)}, bf16[2048,1024]{1,0:T(8,128)(2,1)}, u32[]{:S(2)}) copy-start(bf16[2048,1024]{1,0:T(8,128)(2,1)} %param.13) | copy-start | bytes 12582916
Sparse Core Ops, SparseCore 0:
  234.7 104.9 all-gather.1
  735.9 145.9 reduce-scatter.1
where the time goes:
time: 894 us; the launch traced here: 889 us
  blocking collectives  369 us (41%)
  waiting for transfers between devices  288 us (32%)
  matrix products  121 us (14%)
  local copies, waits for them, and re-layouts  44 us (5%)
  other arithmetic  39.2 us (4%)
  between operations  14.7 us (2%)
  starting transfers between devices  13.6 us (2%)
    all_to_all x1, blocking collectives, per_device(): lax.all_to_all(gathered, 'tm', split_axis=1, concat_axis=0, tiled=True)  369 us
    reduce_scatter x1, waiting for transfers between devices, per_device(): lax.psum_scatter(jnp.dot(regrouped, calibration, preferred_element_type=j...  146 us
    all_gather x1, waiting for transfers between devices, per_device(): gathered = lax.all_gather(aligned, 'col', axis=1, tiled=True)  105 us
    dot_general x4, matrix products, per_device(): lax.dot_general(upper_part, place_onehot, dims, preferred_element_type=jn...  51 us
    dot_general x4, matrix products, per_device(): lax.dot_general(lower_part, place_onehot, dims, preferred_element_type=jn...  48.6 us
    all_to_all x1, waiting for transfers between devices, per_device(): lax.all_to_all(outgoing, 'tm', split_axis=0, concat_axis=0, tiled=True)  36.4 us
    dot_general x1, matrix products, per_device(): jnp.dot(regrouped, calibration, preferred_element_type=jnp.float32)  19.3 us
  transfers between devices with their start and end apart: 4, of which 3 were waited for; matrix products, arithmetic and copies ran while one was open for 5% of the time, Pallas kernels for 0%

commit v1 on v0

v1 whole, which is shorter than its diff:
```python
import functools

import jax
import jax.numpy as jnp
from jax import lax
from jax.experimental import pallas as pl
from jax.experimental.pallas import tpu as pltpu
from jax.sharding import PartitionSpec as P

ROWS_DEV = 512
CHUNK = 256
UNROLL = 8


def spread_samples(values, shifts):
    samples = values.astype(jnp.float32)
    offsets = shifts.astype(jnp.float32)
    result = jnp.zeros(samples.shape, jnp.float32)
    lead = [(0, 0)] * (samples.ndim - 1)
    for displace in (-1, 0, 1):
        weight = jnp.maximum(0.0, 1.0 - jnp.abs(offsets - displace)).astype(jnp.bfloat16)
        weight = lax.optimization_barrier(weight).astype(jnp.float32)
        product = weight * samples
        if displace == 1:
            result = result + jnp.pad(product[..., :-1], lead + [(1, 0)])
        elif displace == -1:
            result = jnp.pad(product[..., 1:], lead + [(0, 1)])
        else:
            result = result + product
    return result


def project_kernel(
    cfg, sens_ref, off_ref, contrib_hbm, *rest
):
    parts, sources, stride, rows, bins, capacity = cfg
    calib_hbm = rest[:parts]
    out_ref = rest[parts]
    contrib_bf, contrib, calib, gathered, picked, total, sems = rest[parts + 1:]
    copies = [pltpu.make_async_copy(contrib_hbm, contrib_bf, sems.at[parts])]
    for part in range(parts):
        copies.append(
            pltpu.make_async_copy(
                calib_hbm[part], calib.at[pl.ds(part * rows, rows)], sems.at[part]
            )
        )
    for copy in copies:
        copy.start()
    width = calib.shape[1]
    room = gathered.shape[0]
    gathered[...] = jnp.zeros_like(gathered)
    picked[...] = jnp.zeros_like(picked)
    copies[0].wait()
    piece = 256
    whole = sources * stride // piece

    def widen(step, carry):
        at = pl.ds(pl.multiple_of(step * piece, piece), piece)
        contrib[at, :] = contrib_bf[at, :].astype(jnp.float32)
        return carry

    lax.fori_loop(0, whole, widen, 0)
    if whole * piece < sources * stride:
        tail = pl.ds(whole * piece, sources * stride - whole * piece)
        contrib[tail, :] = contrib_bf[tail, :].astype(jnp.float32)
    for copy in copies[1:]:
        copy.wait()

    def flush(count):
        def chunk(step, carry):
            start = pl.multiple_of(step * CHUNK, CHUNK)
            row = lax.broadcasted_iota(jnp.int32, (CHUNK, picked.shape[1]), 0) + start
            left = jnp.where(row < count, picked[pl.ds(start, CHUNK), :], 0.0).astype(jnp.bfloat16)
            right = jnp.concatenate(
                [gathered[pl.ds(start, CHUNK), lane, :].astype(jnp.bfloat16) for lane in range(width)],
                axis=1,
            )
            total[...] += lax.dot_general(
                left, right, (((0,), (0,)), ((), ())), preferred_element_type=jnp.float32
            )
            return carry

        lax.fori_loop(0, (count + CHUNK - 1) // CHUNK, chunk, 0)

    def window(w, carry):
        total[...] = jnp.zeros_like(total)

        def source(src, count):
            begin = off_ref[src * (bins + 1) + w]
            end = off_ref[src * (bins + 1) + w + 1]
            base = src * stride + begin

            def copy_rows(step, inner):
                for lane in range(UNROLL):
                    at = step * UNROLL + lane
                    sensor = sens_ref[base + at]
                    gathered[count + at] = calib[sensor].astype(jnp.float32)
                    picked[pl.ds(count + at, 1), :] = contrib[pl.ds(base + at, 1), :]
                return inner

            lax.fori_loop(0, (end - begin + UNROLL - 1) // UNROLL, copy_rows, 0)
            count = count + end - begin
            full = count + capacity + UNROLL > room

            @pl.when(full)
            def _():
                flush(count)

            return jnp.where(full, 0, count)

        count = lax.fori_loop(0, sources, source, 0)
        flush(count)
        out_ref[pl.ds(pl.multiple_of(w * 128, 128), 128), :] = total[...].astype(out_ref.dtype)
        return carry

    lax.fori_loop(0, bins, window, 0)


def per_device(
    block_values, block_shifts, block_sensor, block_window, block_owner, block_counts, calibration
):
    values = block_values[0]
    blocks, length = values.shape
    owners = lax.axis_size("tm")
    cols = lax.axis_size("col")
    ratio = owners // cols
    windows = ROWS_DEV // length
    rows, outputs = calibration.shape
    lanes = outputs // 128
    capacity = min(blocks, blocks * 3 // (2 * owners))
    me = lax.axis_index("tm")
    lot = me % ratio

    calib = lax.optimization_barrier(calibration.reshape(rows, lanes, 128))
    calib_parts = [calib]
    for step in range(1, ratio):
        pairs = [
            ((t // ratio) * ratio + (t + step) % ratio, t) for t in range(owners)
        ]
        calib_parts.append(lax.ppermute(calib, "tm", pairs))

    contribution = spread_samples(values, block_shifts[0]).astype(jnp.bfloat16)
    block_index = lax.iota(jnp.int32, blocks)
    is_live = block_index < block_counts[0, 0]
    owner = block_owner[0, :, 0]
    per_lot = owners // ratio * windows
    bin_of = (owner % ratio) * per_lot + (owner // ratio) * windows + block_window[0]
    bin_of = jnp.where(is_live, bin_of, owners * windows)
    order = bin_of * blocks + block_index
    rank = jnp.sum((order[None, :] < order[:, None]).astype(jnp.int32), axis=1)
    place = (rank[None, :] == block_index[:, None]).astype(jnp.bfloat16)
    sensor = block_sensor[0]
    payload = jnp.concatenate(
        (
            contribution,
            (sensor // 128).astype(jnp.bfloat16)[:, None],
            (sensor % 128).astype(jnp.bfloat16)[:, None],
            jnp.zeros((blocks, length - 2), jnp.bfloat16),
        ),
        axis=1,
    )
    placed = jnp.dot(place, payload, preferred_element_type=jnp.float32)
    bounds = jnp.sum(
        (bin_of[None, :] < lax.iota(jnp.int32, owners * windows + 1)[:, None]).astype(jnp.int32), axis=1
    )
    bound_rows = -(-(owners * windows + 1) // length)
    bounds = jnp.pad(bounds, (0, bound_rows * length - bounds.shape[0]))
    extra = jnp.concatenate(
        (
            placed[:, length].reshape(-1, length),
            placed[:, length + 1].reshape(-1, length),
            (bounds // 128).astype(jnp.float32).reshape(-1, length),
            (bounds % 128).astype(jnp.float32).reshape(-1, length),
        ),
        axis=0,
    )
    extra_rows = -(-extra.shape[0] // 16) * 16
    extra = jnp.pad(extra, ((0, extra_rows - extra.shape[0]), (0, 0)))
    parcel = jnp.concatenate((placed[:, :length], extra), axis=0).astype(jnp.bfloat16)
    stride = blocks + extra_rows
    swap = [
        (t * cols + c, (c * ratio + t % ratio) * cols + t // ratio)
        for t in range(owners)
        for c in range(cols)
    ]
    parcel = lax.ppermute(parcel, ("tm", "col"), swap)
    steps = [parcel]
    for step in range(1, ratio):
        pairs = [
            ((t // ratio) * ratio + (t + step) % ratio, t) for t in range(owners)
        ]
        steps.append(lax.ppermute(parcel, "tm", pairs))
    bundle = jnp.concatenate(steps, axis=0)
    bundle = lax.all_gather(bundle, "col", axis=0, tiled=True)
    sources = owners

    meta = bundle.reshape(sources, stride, length)[:, blocks:].astype(jnp.int32)
    third = blocks // length
    sensors = (meta[:, :third] * 128 + meta[:, third:2 * third]).reshape(sources, blocks)
    sensors = ((sensors // rows - lot) % ratio) * rows + sensors % rows
    sensors = jnp.pad(sensors, ((0, 0), (0, extra_rows))).reshape(-1)
    limit = (
        meta[:, 2 * third:2 * third + bound_rows] * 128
        + meta[:, 2 * third + bound_rows:2 * third + 2 * bound_rows]
    ).reshape(sources, bound_rows * length)
    limit = lax.dynamic_slice_in_dim(limit, lot * per_lot, per_lot + 1, axis=1).reshape(-1)

    room = -(-(CHUNK * 4 + capacity + 2 * UNROLL) // CHUNK) * CHUNK
    total_rows = sources * stride
    any_space = pl.BlockSpec(memory_space=pl.ANY)
    smem = pl.BlockSpec(memory_space=pltpu.SMEM)
    cfg = (ratio, sources, stride, rows, per_lot, capacity)
    partial = pl.pallas_call(
        functools.partial(project_kernel, cfg),
        out_shape=jax.ShapeDtypeStruct((per_lot * length, outputs), jnp.bfloat16),
        in_specs=[smem, smem, any_space] + [any_space] * ratio,
        out_specs=pl.BlockSpec(memory_space=pltpu.VMEM),
        scratch_shapes=[
            pltpu.VMEM((total_rows, length), jnp.bfloat16),
            pltpu.VMEM((total_rows, length), jnp.float32),
            pltpu.VMEM((ratio * rows, lanes, 128), jnp.bfloat16),
            pltpu.VMEM((room, lanes, 128), jnp.float32),
            pltpu.VMEM((room, length), jnp.float32),
            pltpu.VMEM((length, outputs), jnp.float32),
            pltpu.SemaphoreType.DMA((ratio + 1,)),
        ],
        compiler_params=pltpu.CompilerParams(vmem_limit_bytes=60 * 1024 * 1024),
        cost_estimate=pl.CostEstimate(flops=6 * 10**9, bytes_accessed=40 * 10**6, transcendentals=0),
    )(sensors, limit, bundle, *calib_parts)
    groups = [[t for t in range(owners) if t % ratio == p] for p in range(ratio)]
    return lax.psum_scatter(
        partial, "tm", scatter_dimension=0, axis_index_groups=groups, tiled=True
    )


def solution(mesh):
    placed = (
        P("col", "tm", None),
        P("col", "tm", None),
        P("col", "tm"),
        P("col", "tm"),
        P("col", "tm", None),
        P("col", "tm"),
        P("tm", "col"),
    )
    return jax.shard_map(
        per_device, mesh=mesh, in_specs=placed, out_specs=P("tm", "col"), check_vma=False
    )
```

time: 894 us -> 319 us (0.36)
  blocking collectives: 369 us -> 0 us
  matrix products: 121 us -> 3.45 us
  waiting for transfers between devices: 288 us -> 204 us
  Pallas kernels: 0 us -> 71.5 us
  local copies, waits for them, and re-layouts: 44 us -> 8.51 us
  other arithmetic: 39.2 us -> 7.65 us
    all_to_all x1 -> x0, blocking collectives: 369 us -> none  [per_device(): lax.all_to_all(gathered, 'tm', split_axis=1, concat_axis=0, tiled=True)]
    dot_general x10 -> x1, matrix products: 121 us -> 3.45 us  [per_device(): placed = jnp.dot(place, payload, preferred_element_type=jnp.float32)]
    pallas_call x0 -> x1, Pallas kernels: none -> 71.5 us  [per_device(): pl.pallas_call(functools.partial(project_kernel, cfg), out_shape=jax.Shap...]
    all_gather x1, waiting for transfers between devices: 105 us -> 58.8 us  [per_device(): bundle = lax.all_gather(bundle, 'col', axis=0, tiled=True)]
    all_to_all x2 -> x0, waiting for transfers between devices: 36.4 us -> none  [the longest x1 36.4 us: per_device(): lax.all_to_all(outgoing, 'tm', split_axis=0, concat_axis=0, tiled=True)]
    reduce_scatter x1, waiting for transfers between devices: 146 us -> 118 us  [per_device(): lax.psum_scatter(partial, 'tm', scatter_dimension=0, axis_index_groups=gr...]
    ppermute x0 -> x3, waiting for transfers between devices: none -> 28 us  [the longest x1 20.7 us: per_device(): calib_parts.append(lax.ppermute(calib, 'tm', pairs))]
    gather x2 -> x0, local copies, waits for them, and re-layouts: 27.8 us -> none  [the longest x1 17.4 us: per_device(): jnp.take(row_keys, source_row, axis=0)]
  transfers between devices with their start and end apart: 4 -> 5, of which waited for: 3 -> 4; matrix products, arithmetic and copies ran while one was open for 5% -> 2% of each run, Pallas kernels for 0% -> 0%
where the time goes in v1:
time: 319 us; the launch traced here: 316 us
  waiting for transfers between devices  204 us (64%)
  Pallas kernels  71.5 us (22%)
  between operations  14.3 us (4%)
  local copies, waits for them, and re-layouts  8.51 us (3%)
  other arithmetic  7.65 us (2%)
  starting transfers between devices  6 us (2%)
  matrix products  3.45 us (1%)
    reduce_scatter x1, waiting for transfers between devices, per_device(): lax.psum_scatter(partial, 'tm', scatter_dimension=0, axis_index_groups=gr...  118 us
    pallas_call x1, Pallas kernels, per_device(): pl.pallas_call(functools.partial(project_kernel, cfg), out_shape=jax.Shap...  71.5 us
    all_gather x1, waiting for transfers between devices, per_device(): bundle = lax.all_gather(bundle, 'col', axis=0, tiled=True)  58.8 us
    ppermute x1, waiting for transfers between devices, per_device(): calib_parts.append(lax.ppermute(calib, 'tm', pairs))  20.7 us
    ppermute x1, waiting for transfers between devices, per_device(): steps.append(lax.ppermute(parcel, 'tm', pairs))  7.29 us
  transfers between devices with their start and end apart: 5, of which 4 were waited for; matrix products, arithmetic and copies ran while one was open for 2% of the time, Pallas kernels for 0%

profile of v1, /device:TPU:0, one launch (start us, length us, event | category | flops | bytes accessed | tf_op | source)
XLA Modules:
  0.0 315.9 jit_solution(9799634940148232099)
XLA Ops:
  6.5 0.0 copy-start.1
  6.5 0.0 all-gather.2.cloned.1.call-start
  7.2 0.7 fusion.53
  8.0 0.3 copy.13
  8.3 0.0 copy-start.2
  8.3 0.0 copy-start.3
  8.4 0.3 copy.12
  8.7 1.1 bitcast_convert_fusion
  9.8 0.0 copy-done.1
  9.8 0.5 fusion.22
  10.4 0.1 pad.37.clone
  10.4 0.0 copy-done.2
  10.4 0.0 copy-done.3
  10.4 0.1 iota_add_fusion
  10.5 1.8 convert_reduce_fusion
  12.3 0.0 copy-start
  12.3 0.5 slice_multiply_fusion.1
  12.8 0.5 copy-done
  13.4 0.4 add_convert_fusion
  13.8 3.4 %fusion.2 = bf16[2048,256]{1,0:T(8,128)(2,1)S(1)} fusion(s32[2048]{0:T(1024)S(1)} %convert_reduce_fusion, bf16[2048,1]{1,0:T(8,128)(2,1)S(1)} %copy.13, bf16[2048,1]{1,0:T(8,128)(2,1)S(1)} %copy.12, bf16[2048,128]{1,0:T(8,128)(2,1)S(1)} %add_convert_fusion, bf16[256]{0:T(256)(128)(2,1)S(1)} %pad.37.clone), kind=kOutput, calls=%fused_computation.4 | convolution fusion | flops 2156396544 | bytes 1589760 | tf_op jit(solution)/shard_map/dot_general | solution.py:162
  17.2 0.6 slice_reduce_fusion.1
  17.8 0.1 convert_reduce_fusion.1
  18.1 0.7 collective-permute-start
  18.8 0.0 collective-permute-done
  18.8 3.1 collective-permute-start.1
  21.8 7.3 %collective-permute-done.1 = bf16[2096,128]{1,0:T(8,128)(2,1)S(1)} collective-permute-done((bf16[2096,128]{1,0:T(8,128)(2,1)S(1)}, bf16[2096,128]{1,0:T(8,128)(2,1)S(1)}, u32[]{:S(2)}, u32[]{:S(2)}) %collective-permute-start.1) | collective-permute-done | bytes 536608 | tf_op jit(solution)/shard_map/ppermute | solution.py:192
  29.1 1.1 pad_maximum_fusion
  30.3 0.0 all-gather.2.cloned.1.call-update
  30.3 0.2 reduce-scatter.2.cloned.1.call-start
  30.5 5.3 %copy.17 = bf16[256,8,8,128]{3,2,1,0:T(8,128)(2,1)} copy(bf16[256,8,8,128]{3,1,2,0:T(8,128)(2,1)} %bitcast.77) | data formatting | bytes 8388608
  35.8 2.0 collective-permute-start.2
  37.8 58.8 %all-gather.2.cloned.1.call-done.contrib_hbm = bf16[16768,128]{1,0:T(8,128)(2,1)} async-done(((bf16[4192,128]{1,0:T(8,128)(2,1)}), bf16[16768,128]{1,0:T(8,128)(2,1)}) %all-gather.2.cloned.1.call-update) | async-done | bytes 4292624 | tf_op jit(solution)/shard_map/all_gather | solution.py:194
  96.6 0.9 slice_convert_fusion
  97.5 0.1 fusion.54
  97.6 0.7 reshape.336.off_ref
  98.3 0.1 fusion.27
  98.4 0.7 reshape.335.sens_ref
  99.1 20.7 %collective-permute-done.2.rest_1_ = bf16[2048,8,128]{2,1,0:T(8,128)(2,1)} collective-permute-done((bf16[2048,8,128]{2,1,0:T(8,128)(2,1)}, bf16[2048,8,128]{2,1,0:T(8,128)(2,1)}, u32[]{:S(2)}, u32[]{:S(2)}) %collective-permute-start.2) | collective-permute-done | bytes 4194336 | tf_op jit(solution)/shard_map/ppermute | solution.py:140
  119.9 71.5 %shard_map.73 = bf16[2048,1024]{1,0:T(8,128)(2,1)} custom-call(s32[16768]{0:T(1024)} %reshape.335.sens_ref, s32[136]{0:T(256)} %reshape.336.off_ref, bf16[16768,128]{1,0:T(8,128)(2,1)} %all-gather.2.cloned.1.call-done.contrib_hbm, bf16[2048,8,128]{2,1,0:T(8,128)(2,1)} %bitcast.20.rest_0_, bf16[2048,8,128]{2,1,0:T(8,128)(2,1)} %collective-permute-done.2.rest_1_), custom_call_target="tpu_custom_call" | custom-call | flops 6000000000 | bytes 40000000 | tf_op jit(solution)/shard_map/pallas_call | solution.py:213
  191.4 0.0 reduce-scatter.2.cloned.1.call-update
  191.4 117.6 %reduce-scatter.2.cloned.1.call-done = bf16[512,1024]{1,0:T(8,128)(2,1)} async-done(((bf16[2048,1024]{1,0:T(8,128)(2,1)}), bf16[512,1024]{1,0:T(8,128)(2,1)}) %reduce-scatter.2.cloned.1.call-update) | async-done | bytes 1048592 | tf_op jit(solution)/shard_map/reduce_scatter | solution.py:231
  (11 shorter events, 0.2 us)
Async XLA Ops:
  6.5 3.3 %copy-start.1 = (bf16[1,2048,128]{2,1,0:T(8,128)(2,1)S(1)}, bf16[1,2048,128]{2,1,0:T(8,128)(2,1)}, u32[]{:S(2)}) copy-start(bf16[1,2048,128]{2,1,0:T(8,128)(2,1)} %param.8) | copy-start | bytes 1572868
  6.5 90.0 %all-gather.2.cloned.1.call-start = ((), (), s32[]{:S(2)}) async-start(), calls=%async_computation.1 | async-start | bytes 5365760 | tf_op jit(solution)/shard_map/all_gather | solution.py:194
  8.3 2.1 copy-start.2
  8.3 2.1 copy-start.3
  12.3 1.0 copy-start
  18.1 0.7 collective-permute-start
  18.8 10.4 %collective-permute-start.1 = (bf16[2096,128]{1,0:T(8,128)(2,1)S(1)}, bf16[2096,128]{1,0:T(8,128)(2,1)S(1)}, u32[]{:S(2)}, u32[]{:S(2)}) collective-permute-start(bf16[2096,128]{1,0:T(8,128)(2,1)S(1)} %collective-permute-done), channel_id=1, source_target_pairs={{4,0},{0,4},{12,8},{8,12},{20,16},{16,20},{28,24},{24,28},{5,1},{1... | collective-permute-start | bytes 1609736 | tf_op jit(solution)/shard_map/ppermute | solution.py:192
  30.3 278.7 %reduce-scatter.2.cloned.1.call-start = ((), (), s32[]{:S(2)}) async-start(), calls=%async_computation.2 | async-start | bytes 5242880 | tf_op jit(solution)/shard_map/reduce_scatter | solution.py:231
  35.8 84.1 %collective-permute-start.2 = (bf16[2048,8,128]{2,1,0:T(8,128)(2,1)}, bf16[2048,8,128]{2,1,0:T(8,128)(2,1)}, u32[]{:S(2)}, u32[]{:S(2)}) collective-permute-start(bf16[2048,8,128]{2,1,0:T(8,128)(2,1)} %bitcast.20.rest_0_), channel_id=1, source_target_pairs={{4,0},{0,4},{12,8},{8,12},{20,16},{16,20},{28,24},{24,28},{5,1},{1... | collective-permute-start | bytes 12582920 | tf_op jit(solution)/shard_map/ppermute | solution.py:140
Sparse Core Ops, SparseCore 0:
  30.4 66.1 all-gather.1
  191.6 117.4 reduce-scatter.1

commit v2 on v1

v2 whole, which is shorter than its diff:
```python
import functools

import jax
import jax.numpy as jnp
from jax import lax
from jax.experimental import pallas as pl
from jax.experimental.pallas import tpu as pltpu
from jax.sharding import PartitionSpec as P


ROWS_DEV = 512
CHUNK = 256
UNROLL = 8
PIECES = 2


def spread_samples(values, shifts):
    samples = values.astype(jnp.float32)
    offsets = shifts.astype(jnp.float32)
    result = jnp.zeros(samples.shape, jnp.float32)
    lead = [(0, 0)] * (samples.ndim - 1)
    for displace in (-1, 0, 1):
        weight = jnp.maximum(0.0, 1.0 - jnp.abs(offsets - displace)).astype(jnp.bfloat16)
        weight = lax.optimization_barrier(weight).astype(jnp.float32)
        product = weight * samples
        if displace == 1:
            result = result + jnp.pad(product[..., :-1], lead + [(1, 0)])
        elif displace == -1:
            result = jnp.pad(product[..., 1:], lead + [(0, 1)])
        else:
            result = result + product
    return result


def project_kernel(cfg, sens_ref, off_ref, *rest):
    sources, stride, heights, windows, owners, pieces, seeded, capacity = cfg
    bins = windows * owners
    share = windows // PIECES
    contrib_hbm, rest = rest[:sources], rest[sources:]
    calib_hbm, rest = rest[:len(heights)], rest[len(heights):]
    seed_refs, rest = (rest[:len(pieces)], rest[len(pieces):]) if seeded else ((), rest)
    out_refs, rest = rest[:len(pieces)], rest[len(pieces):]
    contrib_bf, contrib, calib, gathered, picked, total, sems = rest
    copies = []
    for src in range(sources):
        copies.append(
            pltpu.make_async_copy(
                contrib_hbm[src], contrib_bf.at[pl.ds(src * stride, stride)], sems.at[src]
            )
        )
    at = 0
    for part, height in enumerate(heights):
        copies.append(
            pltpu.make_async_copy(
                calib_hbm[part], calib.at[pl.ds(at, height)], sems.at[sources + part]
            )
        )
        at += height
    for copy in copies:
        copy.start()
    width = calib.shape[1]
    room = gathered.shape[0]
    gathered[...] = jnp.zeros_like(gathered)
    picked[...] = jnp.zeros_like(picked)
    for copy in copies[:sources]:
        copy.wait()

    def widen(step, carry):
        at = pl.ds(pl.multiple_of(step * stride, 16), stride)
        contrib[at, :] = contrib_bf[at, :].astype(jnp.float32)
        return carry

    lax.fori_loop(0, sources, widen, 0)
    for copy in copies[sources:]:
        copy.wait()

    def flush(count):
        def chunk(step, carry):
            start = pl.multiple_of(step * CHUNK, CHUNK)
            row = lax.broadcasted_iota(jnp.int32, (CHUNK, picked.shape[1]), 0) + start
            left = jnp.where(row < count, picked[pl.ds(start, CHUNK), :], 0.0).astype(jnp.bfloat16)
            right = jnp.concatenate(
                [gathered[pl.ds(start, CHUNK), lane, :].astype(jnp.bfloat16) for lane in range(width)],
                axis=1,
            )
            total[...] += lax.dot_general(
                left, right, (((0,), (0,)), ((), ())), preferred_element_type=jnp.float32
            )
            return carry

        lax.fori_loop(0, (count + CHUNK - 1) // CHUNK, chunk, 0)

    for number, index in enumerate(pieces):

        def window(slot, carry, number=number, index=index):
            w = (slot // share) * windows + index * share + slot % share
            rows_at = pl.ds(pl.multiple_of(slot * 128, 128), 128)
            if seeded:
                total[...] = seed_refs[number][rows_at, :]
            else:
                total[...] = jnp.zeros_like(total)

            def source(src, count):
                begin = off_ref[src * (bins + 1) + w]
                end = off_ref[src * (bins + 1) + w + 1]
                base = src * stride + begin

                def copy_rows(step, inner):
                    for lane in range(UNROLL):
                        at = step * UNROLL + lane
                        sensor = sens_ref[base + at]
                        gathered[count + at] = calib[sensor].astype(jnp.float32)
                        picked[pl.ds(count + at, 1), :] = contrib[pl.ds(base + at, 1), :]
                    return inner

                lax.fori_loop(0, (end - begin + UNROLL - 1) // UNROLL, copy_rows, 0)
                count = count + end - begin
                full = count + capacity + UNROLL > room

                @pl.when(full)
                def _():
                    flush(count)

                return jnp.where(full, 0, count)

            flush(lax.fori_loop(0, sources, source, 0))
            out_refs[number][rows_at, :] = total[...].astype(out_refs[number].dtype)
            return carry

        lax.fori_loop(0, owners * share, window, 0)


def project(sensors, limit, parcels, calibs, seeds, pieces, windows, owners, capacity, dtype):
    stride, length = parcels[0].shape
    sources = len(parcels)
    lanes = calibs[0].shape[1]
    outputs = lanes * 128
    heights = tuple(c.shape[0] for c in calibs)
    room = -(-(CHUNK * 4 + capacity + 2 * UNROLL) // CHUNK) * CHUNK
    height = windows // PIECES * owners * length
    any_space = pl.BlockSpec(memory_space=pl.ANY)
    smem = pl.BlockSpec(memory_space=pltpu.SMEM)
    vmem = pl.BlockSpec(memory_space=pltpu.VMEM)
    cfg = (sources, stride, heights, windows, owners, pieces, bool(seeds), capacity)
    return pl.pallas_call(
        functools.partial(project_kernel, cfg),
        out_shape=[jax.ShapeDtypeStruct((height, outputs), dtype)] * len(pieces),
        in_specs=[smem, smem] + [any_space] * (sources + len(calibs)) + [vmem] * len(seeds),
        out_specs=[vmem] * len(pieces),
        scratch_shapes=[
            pltpu.VMEM((sources * stride, length), jnp.bfloat16),
            pltpu.VMEM((sources * stride, length), jnp.float32),
            pltpu.VMEM((sum(heights), lanes, 128), jnp.bfloat16),
            pltpu.VMEM((room, lanes, 128), jnp.float32),
            pltpu.VMEM((room, length), jnp.float32),
            pltpu.VMEM((length, outputs), jnp.float32),
            pltpu.SemaphoreType.DMA((sources + len(calibs),)),
        ],
        compiler_params=pltpu.CompilerParams(vmem_limit_bytes=58 * 1024 * 1024),
        cost_estimate=pl.CostEstimate(
            flops=15 * 10**9 * len(pieces), bytes_accessed=20 * 10**6, transcendentals=0
        ),
    )(sensors, limit, *parcels, *calibs, *seeds)


def resample(
    block_values, block_shifts, block_sensor, block_window, block_owner, block_counts, calibration
):
    values = block_values[0]
    blocks, length = values.shape
    owners = lax.axis_size("tm")
    cols = lax.axis_size("col")
    ratio = owners // cols
    windows = ROWS_DEV // length
    rows, outputs = calibration.shape
    lanes = outputs // 128
    capacity = min(blocks, blocks * 3 // (2 * owners))
    lot = lax.axis_index("tm") % ratio

    def shifted(step):
        return [((t // ratio) * ratio + (t + step) % ratio, t) for t in range(owners)]

    calib = lax.optimization_barrier(calibration.reshape(rows, lanes, 128))
    early = rows // 4
    calib_early = []
    for step in range(1, ratio):
        calib_early.append(lax.ppermute(calib[:early], "tm", shifted(step)))

    contribution = spread_samples(values, block_shifts[0]).astype(jnp.bfloat16)
    block_index = lax.iota(jnp.int32, blocks)
    is_live = block_index < block_counts[0, 0]
    owner = block_owner[0, :, 0]
    sensor = block_sensor[0]
    held = owners // ratio
    per_lot = held * windows
    bins = ratio * ratio * per_lot
    bin_of = ((owner % ratio) * ratio + sensor // rows) * per_lot
    bin_of = bin_of + (owner // ratio) * windows + block_window[0]
    bin_of = jnp.where(is_live, bin_of, bins)
    order = bin_of * blocks + block_index
    rank = jnp.sum((order[None, :] < order[:, None]).astype(jnp.int32), axis=1)
    place = (rank[None, :] == block_index[:, None]).astype(jnp.bfloat16)
    payload = jnp.concatenate(
        (
            contribution,
            (sensor // 128).astype(jnp.bfloat16)[:, None],
            (sensor % 128).astype(jnp.bfloat16)[:, None],
            jnp.zeros((blocks, length - 2), jnp.bfloat16),
        ),
        axis=1,
    )
    placed = jnp.dot(place, payload, preferred_element_type=jnp.float32)
    bounds = jnp.sum(
        (bin_of[None, :] < lax.iota(jnp.int32, bins + 1)[:, None]).astype(jnp.int32), axis=1
    )
    bound_rows = -(-(bins + 1) // length)
    bounds = jnp.pad(bounds, (0, bound_rows * length - bounds.shape[0]))
    extra = jnp.concatenate(
        (
            placed[:, length].reshape(-1, length),
            placed[:, length + 1].reshape(-1, length),
            (bounds // 128).astype(jnp.float32).reshape(-1, length),
            (bounds % 128).astype(jnp.float32).reshape(-1, length),
        ),
        axis=0,
    )
    extra_rows = -(-extra.shape[0] // 16) * 16
    extra = jnp.pad(extra, ((0, extra_rows - extra.shape[0]), (0, 0)))
    parcel = jnp.concatenate((placed[:, :length], extra), axis=0).astype(jnp.bfloat16)
    swap = [
        (t * cols + c, (c * ratio + t % ratio) * cols + t // ratio)
        for t in range(owners)
        for c in range(cols)
    ]
    parcel = lax.ppermute(parcel, ("tm", "col"), swap)
    parcels = [parcel]
    for step in range(1, ratio):
        parcels.append(lax.ppermute(parcel, "tm", shifted(step)))
    calib_late, last = lax.optimization_barrier((calib[early:], parcels[-1]))
    parcels[-1] = last
    calib_rest = []
    for step in range(1, ratio):
        calib_rest.append(lax.ppermute(calib_late, "tm", shifted(step)))
    bit = 2
    while bit < cols:
        pairs = [(c, c ^ bit) for c in range(cols)]
        parcels += [lax.ppermute(p, "col", pairs) for p in parcels]
        bit *= 2
    pairs = [(c, c ^ 1) for c in range(cols)]
    parcels += [lax.ppermute(p, "col", pairs) for p in parcels]
    sources = len(parcels)

    meta = jnp.stack([p[blocks:] for p in parcels]).astype(jnp.int32)
    third = blocks // length
    sensors = (meta[:, :third] * 128 + meta[:, third:2 * third]).reshape(sources, blocks) % rows
    sensors = jnp.pad(sensors, ((0, 0), (0, extra_rows))).reshape(-1)
    limit = (
        meta[:, 2 * third:2 * third + bound_rows] * 128
        + meta[:, 2 * third + bound_rows:2 * third + 2 * bound_rows]
    ).reshape(sources, bound_rows * length)

    def limit_of(step):
        first = (lot * ratio + (lot + step) % ratio) * per_lot
        return lax.dynamic_slice_in_dim(limit, first, per_lot + 1, axis=1).reshape(-1)

    every = tuple(range(PIECES))
    partial = project(
        sensors, limit_of(0), parcels, [calib], [], every, windows, held, capacity, jnp.float32
    )
    groups = [[t for t in range(owners) if t % ratio == p] for p in range(ratio)]
    results = []
    for piece in every:
        held_sum = partial[piece]
        for step in range(1, ratio):
            kind = jnp.bfloat16 if step == ratio - 1 else jnp.float32
            held_sum = project(
                sensors, limit_of(step), parcels, [calib_early[step - 1], calib_rest[step - 1]],
                [held_sum], (piece,), windows, held, capacity, kind
            )[0]
        results.append(
            lax.psum_scatter(
                held_sum, "tm", scatter_dimension=0, axis_index_groups=groups, tiled=True
            )
        )
    return jnp.concatenate(results, axis=0)


def solution(mesh):
    placed = (
        P("col", "tm", None),
        P("col", "tm", None),
        P("col", "tm"),
        P("col", "tm"),
        P("col", "tm", None),
        P("col", "tm"),
        P("tm", "col"),
    )
    return jax.shard_map(
        resample, mesh=mesh, in_specs=placed, out_specs=P("tm", "col"), check_vma=False
    )
```

time: 319 us -> 277 us (0.87)
  waiting for transfers between devices: 204 us -> 87.5 us
  starting transfers between devices: 6 us -> 44 us
  Pallas kernels: 71.5 us -> 106 us
  local copies, waits for them, and re-layouts: 8.51 us -> 12.8 us
    all_gather x1 -> x0, waiting for transfers between devices: 58.8 us -> none  [per_device(): bundle = lax.all_gather(bundle, 'col', axis=0, tiled=True)]
    reduce_scatter x1 -> x2, waiting for transfers between devices: 118 us -> 70.9 us  [resample(): lax.psum_scatter(held_sum, 'tm', scatter_dimension=0, axis_index_groups=g...]
    ppermute x3 -> x10, starting transfers between devices: 5.78 us -> 43.7 us  [the longest x6 37.2 us: resample(): parcels += [lax.ppermute(p, 'col', pairs) for p in parcels]]
    pallas_call x1 -> x3, Pallas kernels: 71.5 us -> 106 us  [project(): pl.pallas_call(functools.partial(project_kernel, cfg), out_shape=[jax.Sha...]
    ppermute x3 -> x10, waiting for transfers between devices: 28 us -> 16.6 us  [the longest x1 10.9 us: resample(): calib_rest.append(lax.ppermute(calib_late, 'tm', shifted(step)))]
  transfers between devices with their start and end apart: 5 -> 12, of which waited for: 4 -> 6; matrix products, arithmetic and copies ran while one was open for 2% -> 3% of each run, Pallas kernels for 0% -> 28%
where the time goes in v2:
time: 277 us; the launch traced here: 276 us
  Pallas kernels  106 us (38%)
  waiting for transfers between devices  87.5 us (32%)
  starting transfers between devices  44 us (16%)
  between operations  14.4 us (5%)
  local copies, waits for them, and re-layouts  12.8 us (5%)
  other arithmetic  7.8 us (3%)
  matrix products  3.44 us (1%)
    pallas_call x3, Pallas kernels, project(): pl.pallas_call(functools.partial(project_kernel, cfg), out_shape=[jax.Sha...  106 us
    reduce_scatter x2, waiting for transfers between devices, resample(): lax.psum_scatter(held_sum, 'tm', scatter_dimension=0, axis_index_groups=g...  70.9 us
    ppermute x6, starting transfers between devices, resample(): parcels += [lax.ppermute(p, 'col', pairs) for p in parcels]  37.2 us
    ppermute x1, waiting for transfers between devices, resample(): calib_rest.append(lax.ppermute(calib_late, 'tm', shifted(step)))  10.9 us
    unnamed x32, local copies, waits for them, and re-layouts  6.38 us
    ppermute x6, waiting for transfers between devices, resample(): parcels += [lax.ppermute(p, 'col', pairs) for p in parcels]  5.61 us
  transfers between devices with their start and end apart: 12, of which 6 were waited for; matrix products, arithmetic and copies ran while one was open for 3% of the time, Pallas kernels for 28%

profile of v2, /device:TPU:0, one launch (start us, length us, event | category | flops | bytes accessed | tf_op | source)
XLA Modules:
  0.0 276.1 jit_solution(6864450196243190589)
XLA Ops:
  7.2 0.7 fusion.51
  8.0 0.3 copy.13
  8.4 0.0 copy-start.5
  8.4 0.3 copy.12
  8.7 1.1 bitcast_convert_fusion
  9.8 0.5 fusion.22
  10.4 0.1 pad.37.clone
  10.5 0.1 iota_add_fusion
  10.6 1.8 convert_reduce_fusion
  12.4 0.5 slice_multiply_fusion.1
  12.9 0.5 copy-done.2
  13.5 0.4 add_convert_fusion
  13.9 3.4 %fusion.2 = bf16[2048,256]{1,0:T(8,128)(2,1)S(1)} fusion(s32[2048]{0:T(1024)S(1)} %convert_reduce_fusion, bf16[2048,1]{1,0:T(8,128)(2,1)S(1)} %copy.13, bf16[2048,1]{1,0:T(8,128)(2,1)S(1)} %copy.12, bf16[2048,128]{1,0:T(8,128)(2,1)S(1)} %add_convert_fusion, bf16[256]{0:T(256)(128)(2,1)S(1)} %pad.37.clone), kind=kOutput, calls=%fused_computation.4 | convolution fusion | flops 2156396544 | bytes 1589760 | tf_op jit(solution)/shard_map/dot_general | solution.py:212
  17.3 0.6 slice_reduce_fusion.1
  17.9 0.2 convert_reduce_fusion.1
  18.2 1.5 collective-permute-start
  19.6 3.0 %collective-permute-start.1 = (bf16[2096,128]{1,0:T(8,128)(2,1)}, bf16[2096,128]{1,0:T(8,128)(2,1)}, u32[]{:S(2)}, u32[]{:S(2)}) collective-permute-start(bf16[2096,128]{1,0:T(8,128)(2,1)} %collective-permute-done.rest_0_), channel_id=1, source_target_pairs={{4,0},{0,4},{12,8},{8,12},{20,16},{16,20},{28,24},{24,28},{5,1},{1... | collective-permute-start | bytes 1609736 | tf_op jit(solution)/shard_map/ppermute | solution.py:238
  22.6 30.0 %collective-permute-start.2 = (bf16[2096,128]{1,0:T(8,128)(2,1)}, bf16[2096,128]{1,0:T(8,128)(2,1)}, u32[]{:S(2)}, u32[]{:S(2)}) collective-permute-start(bf16[2096,128]{1,0:T(8,128)(2,1)} %collective-permute-done.rest_0_), channel_id=1, source_target_pairs={{0,2},{1,3},{2,0},{3,1},{4,6},{5,7},{6,4},{7,5},{8,10},{9,11},{10,... | collective-permute-start | bytes 1609736 | tf_op jit(solution)/shard_map/ppermute | solution.py:247
  52.7 1.1 copy.16
  53.8 2.0 copy-done
  55.7 1.0 slice.98
  56.8 0.5 collective-permute-start.8
  57.3 2.0 slice.87
  59.3 6.1 %collective-permute-start.3 = (bf16[2096,128]{1,0:T(8,128)(2,1)}, bf16[2096,128]{1,0:T(8,128)(2,1)S(1)}, u32[]{:S(2)}, u32[]{:S(2)}) collective-permute-start(bf16[2096,128]{1,0:T(8,128)(2,1)} %collective-permute-done.1.rest_1_), channel_id=1, source_target_pairs={{0,2},{1,3},{2,0},{3,1},{4,6},{5,7},{6,4},{7,5},{8,10},{9,11},{10,... | collective-permute-start | bytes 1609736 | tf_op jit(solution)/shard_map/ppermute | solution.py:247
  65.4 0.7 constant_dynamic-update-slice_fusion.7
  66.2 0.5 collective-permute-start.5
  66.7 0.7 constant_dynamic-update-slice_fusion.6
  67.4 1.5 collective-permute-start.9
  68.9 0.7 constant_dynamic-update-slice_fusion.5
  69.6 3.3 %collective-permute-done.3.rest_3_ = bf16[2096,128]{1,0:T(8,128)(2,1)S(1)} collective-permute-done((bf16[2096,128]{1,0:T(8,128)(2,1)}, bf16[2096,128]{1,0:T(8,128)(2,1)S(1)}, u32[]{:S(2)}, u32[]{:S(2)}) %collective-permute-start.3) | collective-permute-done | bytes 536608 | tf_op jit(solution)/shard_map/ppermute | solution.py:247
  73.0 0.6 collective-permute-start.7
  73.6 1.5 collective-permute-done.6.rest_6_
  75.1 0.8 collective-permute-done.7.rest_7_
  75.9 0.1 dynamic-slice_reduce_fusion
  76.1 0.6 copy-done.11
  76.7 0.6 reshape.364.off_ref
  77.3 0.7 reshape.362.sens_ref
  78.1 49.6 %shard_map.73 = (f32[1024,1024]{1,0:T(8,128)}, f32[1024,1024]{1,0:T(8,128)}) custom-call(s32[16768]{0:T(1024)} %reshape.362.sens_ref, s32[136]{0:T(256)} %reshape.364.off_ref, bf16[2096,128]{1,0:T(8,128)(2,1)} %collective-permute-done.rest_0_, bf16[2096,128]{1,0:T(8,128)(2,1)} %collective-permute-done.1.rest_1_, ...), custom_call_target="tpu_custom_call" | custom-call | flops 30000001024 | bytes 20000000 | tf_op jit(solution)/shard_map/pallas_call | solution.py:145
  127.7 0.6 reshape.363.off_ref
  128.3 10.9 %collective-permute-done.9.rest_9_ = bf16[1536,8,128]{2,1,0:T(8,128)(2,1)} collective-permute-done((bf16[1536,8,128]{2,1,0:T(8,128)(2,1)S(1)}, bf16[1536,8,128]{2,1,0:T(8,128)(2,1)}, u32[]{:S(2)}, u32[]{:S(2)}) %collective-permute-start.9) | collective-permute-done | bytes 3145760 | tf_op jit(solution)/shard_map/ppermute | solution.py:243
  139.3 28.3 %shard_map.75 = bf16[1024,1024]{1,0:T(8,128)(2,1)} custom-call(s32[16768]{0:T(1024)} %reshape.362.sens_ref, s32[136]{0:T(256)} %reshape.363.off_ref, bf16[2096,128]{1,0:T(8,128)(2,1)} %collective-permute-done.rest_0_, bf16[2096,128]{1,0:T(8,128)(2,1)} %collective-permute-done.1.rest_1_, bf16[2096,128]{1,0:T(8,128)(2,1)} %collective-permute-done.2.rest_2_, ...), custom_call_target="tpu_custom_call" | custom-call | flops 15000000512 | bytes 20000000 | tf_op jit(solution)/shard_map/pallas_call | solution.py:145
  167.6 0.0 reduce-scatter.5.cloned.1.call-update
  167.6 0.3 reduce-scatter.3.cloned.1.call-start
  167.9 28.2 %shard_map.74 = bf16[1024,1024]{1,0:T(8,128)(2,1)} custom-call(s32[16768]{0:T(1024)} %reshape.362.sens_ref, s32[136]{0:T(256)} %reshape.363.off_ref, bf16[2096,128]{1,0:T(8,128)(2,1)} %collective-permute-done.rest_0_, bf16[2096,128]{1,0:T(8,128)(2,1)} %collective-permute-done.1.rest_1_, bf16[2096,128]{1,0:T(8,128)(2,1)} %collective-permute-done.2.rest_2_, ...), custom_call_target="tpu_custom_call" | custom-call | flops 15000000512 | bytes 20000000 | tf_op jit(solution)/shard_map/pallas_call | solution.py:145
  196.1 0.0 reduce-scatter.3.cloned.1.call-update
  196.1 25.8 %reduce-scatter.5.cloned.1.call-done = bf16[256,1024]{1,0:T(8,128)(2,1)} async-done(((bf16[1024,1024]{1,0:T(8,128)(2,1)}), bf16[256,1024]{1,0:T(8,128)(2,1)}) %reduce-scatter.5.cloned.1.call-update) | async-done | bytes 524304 | tf_op jit(solution)/shard_map/reduce_scatter | solution.py:281
  221.9 45.1 %reduce-scatter.3.cloned.1.call-done = bf16[256,1024]{1,0:T(8,128)(2,1)} async-done(((bf16[1024,1024]{1,0:T(8,128)(2,1)}), bf16[256,1024]{1,0:T(8,128)(2,1)}) %reduce-scatter.3.cloned.1.call-update) | async-done | bytes 524304 | tf_op jit(solution)/shard_map/reduce_scatter | solution.py:281
  267.0 2.2 pad_maximum_fusion
  (47 shorter events, 0.4 us)
Async XLA Ops:
  6.5 3.3 %copy-start.3 = (bf16[1,2048,128]{2,1,0:T(8,128)(2,1)S(1)}, bf16[1,2048,128]{2,1,0:T(8,128)(2,1)}, u32[]{:S(2)}) copy-start(bf16[1,2048,128]{2,1,0:T(8,128)(2,1)} %param.8) | copy-start | bytes 1572868
  6.5 215.4 %reduce-scatter.5.cloned.1.call-start = ((), (), s32[]{:S(2)}) async-start(), calls=%async_computation.3 | async-start | bytes 2621440 | tf_op jit(solution)/shard_map/reduce_scatter | solution.py:281
  8.3 2.1 copy-start.4
  8.4 2.1 copy-start.5
  8.4 2.1 copy-start.6
  12.4 1.0 copy-start.2
  13.9 38.8 %copy-start.1 = (bf16[2048,1024]{1,0:T(8,128)(2,1)S(1)}, bf16[2048,1024]{1,0:T(8,128)(2,1)}, u32[]{:S(2)}) copy-start(bf16[2048,1024]{1,0:T(8,128)(2,1)} %param.13) | copy-start | bytes 12582916
  18.2 1.5 collective-permute-start
  19.6 39.6 %collective-permute-start.1 = (bf16[2096,128]{1,0:T(8,128)(2,1)}, bf16[2096,128]{1,0:T(8,128)(2,1)}, u32[]{:S(2)}, u32[]{:S(2)}) collective-permute-start(bf16[2096,128]{1,0:T(8,128)(2,1)} %collective-permute-done.rest_0_), channel_id=1, source_target_pairs={{4,0},{0,4},{12,8},{8,12},{20,16},{16,20},{28,24},{24,28},{5,1},{1... | collective-permute-start | bytes 1609736 | tf_op jit(solution)/shard_map/ppermute | solution.py:238
  22.6 44.7 %collective-permute-start.2 = (bf16[2096,128]{1,0:T(8,128)(2,1)}, bf16[2096,128]{1,0:T(8,128)(2,1)}, u32[]{:S(2)}, u32[]{:S(2)}) collective-permute-start(bf16[2096,128]{1,0:T(8,128)(2,1)} %collective-permute-done.rest_0_), channel_id=1, source_target_pairs={{0,2},{1,3},{2,0},{3,1},{4,6},{5,7},{6,4},{7,5},{8,10},{9,11},{10,... | collective-permute-start | bytes 1609736 | tf_op jit(solution)/shard_map/ppermute | solution.py:247
  53.8 2.0 copy-start
  56.8 71.6 %collective-permute-start.8 = (bf16[512,8,128]{2,1,0:T(8,128)(2,1)}, bf16[512,8,128]{2,1,0:T(8,128)(2,1)}, u32[]{:S(2)}, u32[]{:S(2)}) collective-permute-start(bf16[512,8,128]{2,1,0:T(8,128)(2,1)} %slice.98), channel_id=1, source_target_pairs={{4,0},{0,4},{12,8},{8,12},{20,16},{16,20},{28,24},{24,28},{5,1},{1... | collective-permute-start | bytes 3145736 | tf_op jit(solution)/shard_map/ppermute | solution.py:187
  59.3 13.6 %collective-permute-start.3 = (bf16[2096,128]{1,0:T(8,128)(2,1)}, bf16[2096,128]{1,0:T(8,128)(2,1)S(1)}, u32[]{:S(2)}, u32[]{:S(2)}) collective-permute-start(bf16[2096,128]{1,0:T(8,128)(2,1)} %collective-permute-done.1.rest_1_), channel_id=1, source_target_pairs={{0,2},{1,3},{2,0},{3,1},{4,6},{5,7},{6,4},{7,5},{8,10},{9,11},{10,... | collective-permute-start | bytes 1609736 | tf_op jit(solution)/shard_map/ppermute | solution.py:247
  66.2 6.8 %collective-permute-start.4 = (bf16[2096,128]{1,0:T(8,128)(2,1)}, bf16[2096,128]{1,0:T(8,128)(2,1)S(1)}, u32[]{:S(2)}, u32[]{:S(2)}) collective-permute-start(bf16[2096,128]{1,0:T(8,128)(2,1)} %collective-permute-done.rest_0_), channel_id=1, source_target_pairs={{0,1},{1,0},{2,3},{3,2},{4,5},{5,4},{6,7},{7,6},{8,9},{9,8},{10,11... | collective-permute-start | bytes 1609736 | tf_op jit(solution)/shard_map/ppermute | solution.py:250
  66.2 7.4 %collective-permute-start.5 = (bf16[2096,128]{1,0:T(8,128)(2,1)}, bf16[2096,128]{1,0:T(8,128)(2,1)S(1)}, u32[]{:S(2)}, u32[]{:S(2)}) collective-permute-start(bf16[2096,128]{1,0:T(8,128)(2,1)} %collective-permute-done.1.rest_1_), channel_id=1, source_target_pairs={{0,1},{1,0},{2,3},{3,2},{4,5},{5,4},{6,7},{7,6},{8,9},{9,8},{10,11... | collective-permute-start | bytes 1609736 | tf_op jit(solution)/shard_map/ppermute | solution.py:250
  67.4 71.9 %collective-permute-start.9 = (bf16[1536,8,128]{2,1,0:T(8,128)(2,1)S(1)}, bf16[1536,8,128]{2,1,0:T(8,128)(2,1)}, u32[]{:S(2)}, u32[]{:S(2)}) collective-permute-start(bf16[1536,8,128]{2,1,0:T(8,128)(2,1)S(1)} %slice.87), channel_id=1, source_target_pairs={{4,0},{0,4},{12,8},{8,12},{20,16},{16,20},{28,24},{24,28},{5,1},{1... | collective-permute-start | bytes 9437192 | tf_op jit(solution)/shard_map/ppermute | solution.py:243
  72.9 3.1 %copy-start.7 = (bf16[2096,128]{1,0:T(8,128)(2,1)}, bf16[2096,128]{1,0:T(8,128)(2,1)S(1)}, u32[]{:S(2)}) copy-start(bf16[2096,128]{1,0:T(8,128)(2,1)S(1)} %collective-permute-done.3.rest_3_) | copy-start | bytes 1609732
  72.9 2.1 collective-permute-start.6
  73.0 3.1 %copy-start.8 = (bf16[2096,128]{1,0:T(8,128)(2,1)}, bf16[2096,128]{1,0:T(8,128)(2,1)S(1)}, u32[]{:S(2)}) copy-start(bf16[2096,128]{1,0:T(8,128)(2,1)S(1)} %collective-permute-done.4.rest_4_) | copy-start | bytes 1609732
  73.0 2.9 %collective-permute-start.7 = (bf16[2096,128]{1,0:T(8,128)(2,1)S(1)}, bf16[2096,128]{1,0:T(8,128)(2,1)S(1)}, u32[]{:S(2)}, u32[]{:S(2)}) collective-permute-start(bf16[2096,128]{1,0:T(8,128)(2,1)S(1)} %collective-permute-done.3.rest_3_), channel_id=1, source_target_pairs={{0,1},{1,0},{2,3},{3,2},{4,5},{5,4},{6,7},{7,6},{8,9},{9,8},{10,11... | collective-permute-start | bytes 1609736 | tf_op jit(solution)/shard_map/ppermute | solution.py:250
  73.5 2.5 copy-start.9
  75.1 1.0 copy-start.10
  75.9 0.8 copy-start.11
  167.6 99.5 %reduce-scatter.3.cloned.1.call-start = ((), (), s32[]{:S(2)}) async-start(), calls=%async_computation.2 | async-start | bytes 2621440 | tf_op jit(solution)/shard_map/reduce_scatter | solution.py:281
Sparse Core Ops, SparseCore 0:
  167.7 54.1 reduce-scatter.4
  224.2 42.8 reduce-scatter.2

commit v3 on v2

--- a/solution.py
+++ b/solution.py
@@ -11,6 +11,7 @@
 ROWS_DEV = 512
 CHUNK = 256
 UNROLL = 8
+PITCH = 8
 PIECES = 2
 
 
@@ -59,7 +60,7 @@
     for copy in copies:
         copy.start()
     width = calib.shape[1]
-    room = gathered.shape[0]
+    room = picked.shape[0]
     gathered[...] = jnp.zeros_like(gathered)
     picked[...] = jnp.zeros_like(picked)
     for copy in copies[:sources]:
@@ -80,7 +81,10 @@
             row = lax.broadcasted_iota(jnp.int32, (CHUNK, picked.shape[1]), 0) + start
             left = jnp.where(row < count, picked[pl.ds(start, CHUNK), :], 0.0).astype(jnp.bfloat16)
             right = jnp.concatenate(
-                [gathered[pl.ds(start, CHUNK), lane, :].astype(jnp.bfloat16) for lane in range(width)],
+                [
+                    gathered[pl.ds(start * PITCH + lane, CHUNK, stride=PITCH), :].astype(jnp.bfloat16)
+                    for lane in range(width)
+                ],
                 axis=1,
             )
             total[...] += lax.dot_general(
@@ -109,7 +113,8 @@
                     for lane in range(UNROLL):
                         at = step * UNROLL + lane
                         sensor = sens_ref[base + at]
-                        gathered[count + at] = calib[sensor].astype(jnp.float32)
+                        spot = pl.multiple_of((count + at) * PITCH, PITCH)
+                        gathered[pl.ds(spot, width), :] = calib[sensor].astype(jnp.float32)
                         picked[pl.ds(count + at, 1), :] = contrib[pl.ds(base + at, 1), :]
                     return inner
 
@@ -151,7 +156,7 @@
             pltpu.VMEM((sources * stride, length), jnp.bfloat16),
             pltpu.VMEM((sources * stride, length), jnp.float32),
             pltpu.VMEM((sum(heights), lanes, 128), jnp.bfloat16),
-            pltpu.VMEM((room, lanes, 128), jnp.float32),
+            pltpu.VMEM((room * PITCH, 128), jnp.float32),
             pltpu.VMEM((room, length), jnp.float32),
             pltpu.VMEM((length, outputs), jnp.float32),
             pltpu.SemaphoreType.DMA((sources + len(calibs),)),

time: 277 us -> 266 us (0.960)
  Pallas kernels: 106 us -> 64.8 us
  waiting for transfers between devices: 87.5 us -> 118 us
    pallas_call x3, Pallas kernels: 106 us -> 64.8 us  [project(): pl.pallas_call(functools.partial(project_kernel, cfg), out_shape=[jax.Sha...]
    ppermute x1, waiting for transfers between devices: 10.9 us -> 31.2 us  [resample(): calib_rest.append(lax.ppermute(calib_late, 'tm', shifted(step)))]
    reduce_scatter x2, waiting for transfers between devices: 70.9 us -> 81.7 us  [resample(): lax.psum_scatter(held_sum, 'tm', scatter_dimension=0, axis_index_groups=g...]
  transfers between devices with their start and end apart: 12 -> 12, of which waited for: 6 -> 6; matrix products, arithmetic and copies ran while one was open for 3% -> 3% of each run, Pallas kernels for 28% -> 18%
where the time goes in v3:
time: 266 us
  waiting for transfers between devices  118 us (44%)
  Pallas kernels  64.8 us (24%)
  starting transfers between devices  43.8 us (16%)
  between operations  14.4 us (5%)
  local copies, waits for them, and re-layouts  12.8 us (5%)
  other arithmetic  7.8 us (3%)
  matrix products  3.44 us (1%)
    reduce_scatter x2, waiting for transfers between devices, resample(): lax.psum_scatter(held_sum, 'tm', scatter_dimension=0, axis_index_groups=g...  81.7 us
    pallas_call x3, Pallas kernels, project(): pl.pallas_call(functools.partial(project_kernel, cfg), out_shape=[jax.Sha...  64.8 us
    ppermute x6, starting transfers between devices, resample(): parcels += [lax.ppermute(p, 'col', pairs) for p in parcels]  37.2 us
    ppermute x1, waiting for transfers between devices, resample(): calib_rest.append(lax.ppermute(calib_late, 'tm', shifted(step)))  31.2 us
    unnamed x32, local copies, waits for them, and re-layouts  6.38 us
    ppermute x6, waiting for transfers between devices, resample(): parcels += [lax.ppermute(p, 'col', pairs) for p in parcels]  5.61 us
  transfers between devices with their start and end apart: 12, of which 6 were waited for; matrix products, arithmetic and copies ran while one was open for 3% of the time, Pallas kernels for 18%

profile of v3, /device:TPU:0, one launch (start us, length us, event | category | flops | bytes accessed | tf_op | source)
XLA Modules:
  0.0 265.6 jit_solution(8245894778797682605)
XLA Ops:
  7.2 0.7 fusion.51
  8.0 0.3 copy.13
  8.4 0.0 copy-start.5
  8.4 0.3 copy.12
  8.7 1.1 bitcast_convert_fusion
  9.8 0.5 fusion.22
  10.4 0.1 pad.37.clone
  10.5 0.1 iota_add_fusion
  10.6 1.8 convert_reduce_fusion
  12.4 0.5 slice_multiply_fusion.1
  12.9 0.5 copy-done.2
  13.5 0.4 add_convert_fusion
  13.9 3.4 %fusion.2 = bf16[2048,256]{1,0:T(8,128)(2,1)S(1)} fusion(s32[2048]{0:T(1024)S(1)} %convert_reduce_fusion, bf16[2048,1]{1,0:T(8,128)(2,1)S(1)} %copy.13, bf16[2048,1]{1,0:T(8,128)(2,1)S(1)} %copy.12, bf16[2048,128]{1,0:T(8,128)(2,1)S(1)} %add_convert_fusion, bf16[256]{0:T(256)(128)(2,1)S(1)} %pad.37.clone), kind=kOutput, calls=%fused_computation.4 | convolution fusion | flops 2156396544 | bytes 1589760 | tf_op jit(solution)/shard_map/dot_general | solution.py:217
  17.3 0.6 slice_reduce_fusion.1
  17.9 0.2 convert_reduce_fusion.1
  18.2 1.5 collective-permute-start
  19.6 3.0 %collective-permute-start.1 = (bf16[2096,128]{1,0:T(8,128)(2,1)}, bf16[2096,128]{1,0:T(8,128)(2,1)}, u32[]{:S(2)}, u32[]{:S(2)}) collective-permute-start(bf16[2096,128]{1,0:T(8,128)(2,1)} %collective-permute-done.rest_0_), channel_id=1, source_target_pairs={{4,0},{0,4},{12,8},{8,12},{20,16},{16,20},{28,24},{24,28},{5,1},{1... | collective-permute-start | bytes 1609736 | tf_op jit(solution)/shard_map/ppermute | solution.py:243
  22.6 30.0 %collective-permute-start.2 = (bf16[2096,128]{1,0:T(8,128)(2,1)}, bf16[2096,128]{1,0:T(8,128)(2,1)}, u32[]{:S(2)}, u32[]{:S(2)}) collective-permute-start(bf16[2096,128]{1,0:T(8,128)(2,1)} %collective-permute-done.rest_0_), channel_id=1, source_target_pairs={{0,2},{1,3},{2,0},{3,1},{4,6},{5,7},{6,4},{7,5},{8,10},{9,11},{10,... | collective-permute-start | bytes 1609736 | tf_op jit(solution)/shard_map/ppermute | solution.py:252
  52.7 1.1 copy.16
  53.8 2.0 copy-done
  55.7 1.0 slice.98
  56.8 0.5 collective-permute-start.8
  57.3 2.0 slice.87
  59.3 6.1 %collective-permute-start.3 = (bf16[2096,128]{1,0:T(8,128)(2,1)}, bf16[2096,128]{1,0:T(8,128)(2,1)S(1)}, u32[]{:S(2)}, u32[]{:S(2)}) collective-permute-start(bf16[2096,128]{1,0:T(8,128)(2,1)} %collective-permute-done.1.rest_1_), channel_id=1, source_target_pairs={{0,2},{1,3},{2,0},{3,1},{4,6},{5,7},{6,4},{7,5},{8,10},{9,11},{10,... | collective-permute-start | bytes 1609736 | tf_op jit(solution)/shard_map/ppermute | solution.py:252
  65.4 0.7 constant_dynamic-update-slice_fusion.7
  66.2 0.5 collective-permute-start.5
  66.7 0.7 constant_dynamic-update-slice_fusion.6
  67.4 1.5 collective-permute-start.9
  68.9 0.7 constant_dynamic-update-slice_fusion.5
  69.6 3.3 %collective-permute-done.3.rest_3_ = bf16[2096,128]{1,0:T(8,128)(2,1)S(1)} collective-permute-done((bf16[2096,128]{1,0:T(8,128)(2,1)}, bf16[2096,128]{1,0:T(8,128)(2,1)S(1)}, u32[]{:S(2)}, u32[]{:S(2)}) %collective-permute-start.3) | collective-permute-done | bytes 536608 | tf_op jit(solution)/shard_map/ppermute | solution.py:252
  73.0 0.6 collective-permute-start.7
  73.6 1.5 collective-permute-done.6.rest_6_
  75.1 0.8 collective-permute-done.7.rest_7_
  75.9 0.1 dynamic-slice_reduce_fusion
  76.1 0.6 copy-done.11
  76.7 0.6 reshape.364.off_ref
  77.3 0.7 reshape.362.sens_ref
  78.1 29.4 %shard_map.73 = (f32[1024,1024]{1,0:T(8,128)}, f32[1024,1024]{1,0:T(8,128)}) custom-call(s32[16768]{0:T(1024)} %reshape.362.sens_ref, s32[136]{0:T(256)} %reshape.364.off_ref, bf16[2096,128]{1,0:T(8,128)(2,1)} %collective-permute-done.rest_0_, bf16[2096,128]{1,0:T(8,128)(2,1)} %collective-permute-done.1.rest_1_, ...), custom_call_target="tpu_custom_call" | custom-call | flops 30000001024 | bytes 20000000 | tf_op jit(solution)/shard_map/pallas_call | solution.py:150
  107.5 0.6 reshape.363.off_ref
  108.1 31.2 %collective-permute-done.9.rest_9_ = bf16[1536,8,128]{2,1,0:T(8,128)(2,1)} collective-permute-done((bf16[1536,8,128]{2,1,0:T(8,128)(2,1)S(1)}, bf16[1536,8,128]{2,1,0:T(8,128)(2,1)}, u32[]{:S(2)}, u32[]{:S(2)}) %collective-permute-start.9) | collective-permute-done | bytes 3145760 | tf_op jit(solution)/shard_map/ppermute | solution.py:248
  139.3 17.7 %shard_map.75 = bf16[1024,1024]{1,0:T(8,128)(2,1)} custom-call(s32[16768]{0:T(1024)} %reshape.362.sens_ref, s32[136]{0:T(256)} %reshape.363.off_ref, bf16[2096,128]{1,0:T(8,128)(2,1)} %collective-permute-done.rest_0_, bf16[2096,128]{1,0:T(8,128)(2,1)} %collective-permute-done.1.rest_1_, bf16[2096,128]{1,0:T(8,128)(2,1)} %collective-permute-done.2.rest_2_, ...), custom_call_target="tpu_custom_call" | custom-call | flops 15000000512 | bytes 20000000 | tf_op jit(solution)/shard_map/pallas_call | solution.py:150
  157.0 0.0 reduce-scatter.5.cloned.1.call-update
  157.0 0.0 reduce-scatter.3.cloned.1.call-start
  157.1 17.7 %shard_map.74 = bf16[1024,1024]{1,0:T(8,128)(2,1)} custom-call(s32[16768]{0:T(1024)} %reshape.362.sens_ref, s32[136]{0:T(256)} %reshape.363.off_ref, bf16[2096,128]{1,0:T(8,128)(2,1)} %collective-permute-done.rest_0_, bf16[2096,128]{1,0:T(8,128)(2,1)} %collective-permute-done.1.rest_1_, bf16[2096,128]{1,0:T(8,128)(2,1)} %collective-permute-done.2.rest_2_, ...), custom_call_target="tpu_custom_call" | custom-call | flops 15000000512 | bytes 20000000 | tf_op jit(solution)/shard_map/pallas_call | solution.py:150
  174.8 0.0 reduce-scatter.3.cloned.1.call-update
  174.8 36.5 %reduce-scatter.5.cloned.1.call-done = bf16[256,1024]{1,0:T(8,128)(2,1)} async-done(((bf16[1024,1024]{1,0:T(8,128)(2,1)}), bf16[256,1024]{1,0:T(8,128)(2,1)}) %reduce-scatter.5.cloned.1.call-update) | async-done | bytes 524304 | tf_op jit(solution)/shard_map/reduce_scatter | solution.py:286
  211.3 45.1 %reduce-scatter.3.cloned.1.call-done = bf16[256,1024]{1,0:T(8,128)(2,1)} async-done(((bf16[1024,1024]{1,0:T(8,128)(2,1)}), bf16[256,1024]{1,0:T(8,128)(2,1)}) %reduce-scatter.3.cloned.1.call-update) | async-done | bytes 524304 | tf_op jit(solution)/shard_map/reduce_scatter | solution.py:286
  256.5 2.2 pad_maximum_fusion
  (47 shorter events, 0.4 us)
Async XLA Ops:
  6.5 3.3 %copy-start.3 = (bf16[1,2048,128]{2,1,0:T(8,128)(2,1)S(1)}, bf16[1,2048,128]{2,1,0:T(8,128)(2,1)}, u32[]{:S(2)}) copy-start(bf16[1,2048,128]{2,1,0:T(8,128)(2,1)} %param.8) | copy-start | bytes 1572868
  6.5 204.8 %reduce-scatter.5.cloned.1.call-start = ((), (), s32[]{:S(2)}) async-start(), calls=%async_computation.3 | async-start | bytes 2621440 | tf_op jit(solution)/shard_map/reduce_scatter | solution.py:286
  8.3 2.1 copy-start.4
  8.4 2.1 copy-start.5
  8.4 2.1 copy-start.6
  12.4 1.0 copy-start.2
  13.9 38.8 %copy-start.1 = (bf16[2048,1024]{1,0:T(8,128)(2,1)S(1)}, bf16[2048,1024]{1,0:T(8,128)(2,1)}, u32[]{:S(2)}) copy-start(bf16[2048,1024]{1,0:T(8,128)(2,1)} %param.13) | copy-start | bytes 12582916
  18.2 1.5 collective-permute-start
  19.6 39.6 %collective-permute-start.1 = (bf16[2096,128]{1,0:T(8,128)(2,1)}, bf16[2096,128]{1,0:T(8,128)(2,1)}, u32[]{:S(2)}, u32[]{:S(2)}) collective-permute-start(bf16[2096,128]{1,0:T(8,128)(2,1)} %collective-permute-done.rest_0_), channel_id=1, source_target_pairs={{4,0},{0,4},{12,8},{8,12},{20,16},{16,20},{28,24},{24,28},{5,1},{1... | collective-permute-start | bytes 1609736 | tf_op jit(solution)/shard_map/ppermute | solution.py:243
  22.6 44.7 %collective-permute-start.2 = (bf16[2096,128]{1,0:T(8,128)(2,1)}, bf16[2096,128]{1,0:T(8,128)(2,1)}, u32[]{:S(2)}, u32[]{:S(2)}) collective-permute-start(bf16[2096,128]{1,0:T(8,128)(2,1)} %collective-permute-done.rest_0_), channel_id=1, source_target_pairs={{0,2},{1,3},{2,0},{3,1},{4,6},{5,7},{6,4},{7,5},{8,10},{9,11},{10,... | collective-permute-start | bytes 1609736 | tf_op jit(solution)/shard_map/ppermute | solution.py:252
  53.8 2.0 copy-start
  56.8 51.4 %collective-permute-start.8 = (bf16[512,8,128]{2,1,0:T(8,128)(2,1)}, bf16[512,8,128]{2,1,0:T(8,128)(2,1)}, u32[]{:S(2)}, u32[]{:S(2)}) collective-permute-start(bf16[512,8,128]{2,1,0:T(8,128)(2,1)} %slice.98), channel_id=1, source_target_pairs={{4,0},{0,4},{12,8},{8,12},{20,16},{16,20},{28,24},{24,28},{5,1},{1... | collective-permute-start | bytes 3145736 | tf_op jit(solution)/shard_map/ppermute | solution.py:192
  59.3 13.6 %collective-permute-start.3 = (bf16[2096,128]{1,0:T(8,128)(2,1)}, bf16[2096,128]{1,0:T(8,128)(2,1)S(1)}, u32[]{:S(2)}, u32[]{:S(2)}) collective-permute-start(bf16[2096,128]{1,0:T(8,128)(2,1)} %collective-permute-done.1.rest_1_), channel_id=1, source_target_pairs={{0,2},{1,3},{2,0},{3,1},{4,6},{5,7},{6,4},{7,5},{8,10},{9,11},{10,... | collective-permute-start | bytes 1609736 | tf_op jit(solution)/shard_map/ppermute | solution.py:252
  66.2 6.8 %collective-permute-start.4 = (bf16[2096,128]{1,0:T(8,128)(2,1)}, bf16[2096,128]{1,0:T(8,128)(2,1)S(1)}, u32[]{:S(2)}, u32[]{:S(2)}) collective-permute-start(bf16[2096,128]{1,0:T(8,128)(2,1)} %collective-permute-done.rest_0_), channel_id=1, source_target_pairs={{0,1},{1,0},{2,3},{3,2},{4,5},{5,4},{6,7},{7,6},{8,9},{9,8},{10,11... | collective-permute-start | bytes 1609736 | tf_op jit(solution)/shard_map/ppermute | solution.py:255
  66.2 7.4 %collective-permute-start.5 = (bf16[2096,128]{1,0:T(8,128)(2,1)}, bf16[2096,128]{1,0:T(8,128)(2,1)S(1)}, u32[]{:S(2)}, u32[]{:S(2)}) collective-permute-start(bf16[2096,128]{1,0:T(8,128)(2,1)} %collective-permute-done.1.rest_1_), channel_id=1, source_target_pairs={{0,1},{1,0},{2,3},{3,2},{4,5},{5,4},{6,7},{7,6},{8,9},{9,8},{10,11... | collective-permute-start | bytes 1609736 | tf_op jit(solution)/shard_map/ppermute | solution.py:255
  67.4 71.9 %collective-permute-start.9 = (bf16[1536,8,128]{2,1,0:T(8,128)(2,1)S(1)}, bf16[1536,8,128]{2,1,0:T(8,128)(2,1)}, u32[]{:S(2)}, u32[]{:S(2)}) collective-permute-start(bf16[1536,8,128]{2,1,0:T(8,128)(2,1)S(1)} %slice.87), channel_id=1, source_target_pairs={{4,0},{0,4},{12,8},{8,12},{20,16},{16,20},{28,24},{24,28},{5,1},{1... | collective-permute-start | bytes 9437192 | tf_op jit(solution)/shard_map/ppermute | solution.py:248
  72.9 3.1 %copy-start.7 = (bf16[2096,128]{1,0:T(8,128)(2,1)}, bf16[2096,128]{1,0:T(8,128)(2,1)S(1)}, u32[]{:S(2)}) copy-start(bf16[2096,128]{1,0:T(8,128)(2,1)S(1)} %collective-permute-done.3.rest_3_) | copy-start | bytes 1609732
  72.9 2.1 collective-permute-start.6
  73.0 3.1 %copy-start.8 = (bf16[2096,128]{1,0:T(8,128)(2,1)}, bf16[2096,128]{1,0:T(8,128)(2,1)S(1)}, u32[]{:S(2)}) copy-start(bf16[2096,128]{1,0:T(8,128)(2,1)S(1)} %collective-permute-done.4.rest_4_) | copy-start | bytes 1609732
  73.0 2.9 %collective-permute-start.7 = (bf16[2096,128]{1,0:T(8,128)(2,1)S(1)}, bf16[2096,128]{1,0:T(8,128)(2,1)S(1)}, u32[]{:S(2)}, u32[]{:S(2)}) collective-permute-start(bf16[2096,128]{1,0:T(8,128)(2,1)S(1)} %collective-permute-done.3.rest_3_), channel_id=1, source_target_pairs={{0,1},{1,0},{2,3},{3,2},{4,5},{5,4},{6,7},{7,6},{8,9},{9,8},{10,11... | collective-permute-start | bytes 1609736 | tf_op jit(solution)/shard_map/ppermute | solution.py:255
  73.5 2.5 copy-start.9
  75.1 1.0 copy-start.10
  75.9 0.8 copy-start.11
  157.0 99.5 %reduce-scatter.3.cloned.1.call-start = ((), (), s32[]{:S(2)}) async-start(), calls=%async_computation.2 | async-start | bytes 2621440 | tf_op jit(solution)/shard_map/reduce_scatter | solution.py:286
Sparse Core Ops, SparseCore 0:
  157.1 54.1 reduce-scatter.4
  213.6 42.8 reduce-scatter.2
